TPU v7x, 256 devices: a whole 4x4x8 slice. The times are simulated.
256 devices in a mesh: prow: 16 (over y, x), pcol: 16 (over z, core).
Axes of the slice: x: 4, y: 4, z: 8, core: 2. Of those that a mesh axis runs over, the one named last changes fastest.
Arguments:
- matrix: float32 [4, 16, 256, 4, 16, 256], P(None, 'prow', None, None, 'pcol'), may hold values from -6 to 6, as said below
- factor: float32 [4, 16, 256, 4, 16, 256], P(None, 'prow', None, None, 'pcol'), may hold values from -3 to 3, as said below
Outputs:
- reduced: float32 [4, 16, 256, 4, 16, 256], P(None, 'prow', None, None, 'pcol')
Inputs may be any that keep to these rules, and one draw needn't show every extreme that they name: Symmetric matrix stored in its lower triangle: every entry above the diagonal is zero. `factor`: lower triangular with diagonal entries between 1 and 3; every entry above the diagonal is zero.
All inputs are finite; a program needn't handle non-finite values.
Results may differ from a plain program's by a relative error of at most 0.0001.
Values sent between devices are 32-bit elements; how exact they have to be, the bound alone decides.
No kernel may reach another device: no remote copies, remote signals or barrier semaphores. Data moves between devices by JAX's collectives and lax.ppermute only.
A program may use at most 128 MiB of HBM per device.

v0:
```python
import jax
import jax.numpy as jnp
from jax import lax
from jax.sharding import Mesh
from jax.sharding import PartitionSpec as P

BLOCKS = 2
PCOL = ("pcol_0", "pcol_1")
highest = lax.Precision.HIGHEST


def picked_2(value, axis, root):
    return lax.dynamic_index_in_dim(lax.all_gather(value, axis), root, 0, keepdims=False)


def from_root(value, axes, root):
    value = jnp.where(lax.axis_index(axes) == root, value, jnp.zeros_like(value))
    for axis in axes:
        value = lax.psum(value, axis)
    return value


def product(left, right):
    return jnp.dot(left, right, precision=highest, preferred_element_type=jnp.float32)


def product_trans(left, right):
    return lax.dot_general(
        left, right, (((1,), (1,)), ((), ())), precision=highest, preferred_element_type=jnp.float32
    )


def diagonal_core(diag_block, diag_factor, width):
    identity = jnp.eye(width, dtype=jnp.float32)
    inverse = lax.linalg.triangular_solve(diag_factor, identity, left_side=True, lower=True)
    symmetric = diag_block + diag_block.T - jnp.diag(jnp.diagonal(diag_block))
    inner = product_trans(product(inverse, symmetric), inverse)
    return (inverse, 0.5 * (inner + inner.T))


def on_device(matrix, factor):
    row_tiles = matrix.shape[0]
    width = matrix.shape[2]
    col_tiles = matrix.shape[3]
    prow_count = lax.axis_size("prow")
    pcol_count = lax.axis_size(PCOL)
    prow_index = lax.axis_index("prow")
    pcol_index = lax.axis_index(PCOL)
    height = row_tiles * width
    local = matrix.reshape(height, col_tiles * width)
    factor_local = factor.reshape(height, col_tiles * width)
    tile_rows = jnp.arange(row_tiles, dtype=jnp.int32) * prow_count + prow_index
    tile_cols = jnp.arange(col_tiles, dtype=jnp.int32) * pcol_count + pcol_index
    offsets = jnp.arange(width, dtype=jnp.int32)
    elem_rows = (tile_rows[:, None] * width + offsets[None, :]).reshape(height)
    elem_cols = (tile_cols[:, None] * width + offsets[None, :]).reshape(col_tiles * width)
    lower_part = elem_rows[:, None] >= elem_cols[None, :]
    row_tile_of = jnp.repeat(tile_rows, width)[:, None]
    ratio = pcol_count // prow_count
    home = pcol_index % prow_count

    def select_columns(block):
        shaped = block.reshape(col_tiles, ratio, width, width)
        picked = lax.dynamic_index_in_dim(shaped, pcol_index // prow_count, 1, keepdims=False)
        return picked.reshape(col_tiles * width, width)

    for step in range(BLOCKS):
        owner_row = step % prow_count
        owner_col = step % pcol_count
        first = step // pcol_count * width
        diag_start = step // prow_count * width
        panel = local[:, first : first + width]
        factor_panel = factor_local[:, first : first + width]
        diag_block, diag_factor = (
            picked_2(panel[diag_start : diag_start + width], "prow", owner_row),
            picked_2(factor_panel[diag_start : diag_start + width], "prow", owner_row),
        )
        inverse, core = diagonal_core(diag_block, diag_factor, width)
        below = row_tile_of > step
        factor_rows = jnp.where(below, factor_panel, 0.0)
        shared = product(factor_rows, core)
        halfway = jnp.where(below, product_trans(panel, inverse), 0.0) - 0.5 * shared
        finished = halfway - 0.5 * shared
        got_half, got_factor = (
            from_root(halfway, PCOL, owner_col),
            from_root(factor_rows, PCOL, owner_col),
        )
        keeper = prow_index == home
        col_half, col_factor = lax.psum(
            (
                jnp.where(keeper, select_columns(got_half), 0.0),
                jnp.where(keeper, select_columns(got_factor), 0.0),
            ),
            "prow",
        )
        update = product_trans(
            jnp.concatenate([got_half, got_factor], 1), jnp.concatenate([col_factor, col_half], 1)
        )
        local = local - jnp.where(lower_part, update, 0.0)
        current = local[:, first : first + width]
        diag_rows = jnp.tile(jnp.tril(core), (row_tiles, 1))
        column = jnp.where(row_tile_of == step, diag_rows, jnp.where(below, finished, current))
        column = jnp.where(pcol_index == owner_col, column, current)
        local = local.at[:, first : first + width].set(column)
    return local.reshape(row_tiles, 1, width, col_tiles, 1, width)


def solution(mesh):
    torus = Mesh(mesh.devices.reshape(mesh.shape["prow"], 8, 2), ("prow", "pcol_0", "pcol_1"))
    in_specs = (P(None, "prow", None, None, PCOL, None), P(None, "prow", None, None, PCOL, None))
    out_specs = P(None, "prow", None, None, PCOL, None)
    return jax.shard_map(
        on_device, mesh=torus, in_specs=in_specs, out_specs=out_specs, check_vma=False
    )
```

profile of v0, /device:TPU:2, one launch (start us, length us, event | category | flops | bytes accessed | tf_op | source)
XLA Modules:
  0.0 747.6 jit_solution(9152688396294790002)
XLA Ops:
  6.5 14.3 %reduce.9 = f32[4,256,4,256]{3,2,1,0:T(4,128)} reduce(f32[4,1,256,4,1,256]{5,4,3,2,1,0:T(1,128)} %param.8, f32[]{:T(128)} %constant.193), dimensions={1,4}, to_apply=%param.8.reduce_sub_computation | reduce | bytes 8388612 | tf_op args[0]
  20.8 3.2 copy.35
  26.8 14.2 %reduce.10 = f32[4,256,4,256]{3,2,1,0:T(4,128)} reduce(f32[4,1,256,4,1,256]{5,4,3,2,1,0:T(1,128)} %param.9, f32[]{:T(128)} %constant.193), dimensions={1,4}, to_apply=%param.9.reduce_sub_computation | reduce | bytes 8388612 | tf_op args[1]
  41.1 3.3 copy.38
  47.6 2.8 fusion.20
  50.3 36.0 %all-gather.9.cloned.1.call-done = f32[4096,256]{1,0:T(8,128)} async-done(((f32[256,256]{1,0:T(8,128)}), f32[4096,256]{1,0:T(8,128)}) %all-gather.9.cloned.1.call-update) | async-done | bytes 4194320 | tf_op jit(solution)/shard_map/all_gather | solution.py:13
  87.4 57.5 %all-gather.7.cloned.1.call-done = f32[4096,256]{1,0:T(8,128)} async-done(((f32[256,256]{1,0:T(8,128)}), f32[4096,256]{1,0:T(8,128)}) %all-gather.7.cloned.1.call-update) | async-done | bytes 4194320 | tf_op jit(solution)/shard_map/all_gather | solution.py:13
  146.8 4.1 while.6
  150.9 19.7 %custom-call.8 = f32[2,128,128]{1,2,0:T(8,128)S(1)} custom-call(f32[2,128,128]{2,1,0:T(8,128)S(1)} %get-tuple-element.44), custom_call_target="InvertDiagBlocksLowerTriangular" | custom-call | tf_op jit(solution)/shard_map/triangular_solve/custom-call.1 | solution.py:35
  171.6 2.3 gather_fusion
  175.9 2.3 convolution_multiply_fusion.1
  178.6 2.3 fusion.15
  182.2 2.3 broadcast_select_fusion.5
  184.6 80.9 %all-reduce.19.cloned.1.call-done = (f32[1024,256]{1,0:T(8,128)}, f32[1024,256]{1,0:T(8,128)}) async-done(((f32[1024,256]{1,0:T(8,128)}, f32[1024,256]{1,0:T(8,128)}), (f32[1024,256]{1,0:T(8,128)}, f32[1024,256]{1,0:T(8,128)})) %all-reduce.19.cloned.1.call-update) | async-done | bytes 2097168 | tf_op jit(solution)/shard_map/psum | solution.py:19
  265.6 33.6 %all-reduce.23.cloned.1.call-done = (f32[1024,256]{1,0:T(8,128)}, f32[1024,256]{1,0:T(8,128)}) async-done(((f32[1024,256]{1,0:T(8,128)}, f32[1024,256]{1,0:T(8,128)}), (f32[1024,256]{1,0:T(8,128)}, f32[1024,256]{1,0:T(8,128)})) %all-reduce.23.cloned.1.call-update) | async-done | bytes 2097168 | tf_op jit(solution)/shard_map/psum | solution.py:19
  304.0 101.4 %all-reduce.15.cloned.1.call-done = (f32[1024,256]{1,0:T(8,128)}, f32[1024,256]{1,0:T(8,128)}) async-done(((f32[1024,256]{1,0:T(8,128)}, f32[1024,256]{1,0:T(8,128)}), (f32[1024,256]{1,0:T(8,128)}, f32[1024,256]{1,0:T(8,128)})) %all-reduce.15.cloned.1.call-update) | async-done | bytes 2097168 | tf_op jit(solution)/shard_map/psum | solution.py:89
  405.4 10.8 %fusion = f32[1024,1024]{1,0:T(8,128)S(1)} fusion(f32[1024,1024]{1,0:T(8,128)} %bitcast.90, f32[1024,256]{1,0:T(8,128)} %get-tuple-element.72, f32[1024,256]{1,0:T(8,128)} %get-tuple-element.73, f32[1024,256]{1,0:T(8,128)} %get-tuple-element.64, f32[1024,256]{1,0:T(8,128)} %get-tuple-element.65, s32[1024]{0:T(1024)S(1)} %bitcast.99, s32[1024]{0:T(1024)S(1)} %bitcast.101), kind=kOutput, calls=%fused_computation.8 | convolution fusion | flops 6446645248 | bytes 12591104 | tf_op jit(solution)/shard_map/dot_general | solution.py:28
  419.7 2.7 select_select_fusion.1
  423.4 5.9 while.7
  424.1 2.3 bitcast_dynamic-update-slice_fusion.5
  429.3 19.7 %custom-call.9 = f32[2,128,128]{1,2,0:T(8,128)S(1)} custom-call(f32[2,128,128]{2,1,0:T(8,128)S(1)} %get-tuple-element.45), custom_call_target="InvertDiagBlocksLowerTriangular" | custom-call | tf_op jit(solution)/shard_map/triangular_solve/custom-call.1 | solution.py:35
  450.9 33.9 %all-gather.11.cloned.1.call-done = f32[4096,256]{0,1:T(8,128)} async-done(((f32[256,256]{0,1:T(8,128)}), f32[4096,256]{0,1:T(8,128)}) %all-gather.11.cloned.1.call-update) | async-done | bytes 4194320 | tf_op jit(solution)/shard_map/all_gather | solution.py:13
  485.9 2.4 gather_fusion.1
  490.9 2.3 convolution_multiply_fusion
  493.2 3.9 broadcast_select_fusion.2
  497.2 82.1 %all-reduce.17.cloned.1.call-done = (f32[1024,256]{1,0:T(8,128)}, f32[1024,256]{1,0:T(8,128)}) async-done(((f32[1024,256]{1,0:T(8,128)}, f32[1024,256]{1,0:T(8,128)}), (f32[1024,256]{1,0:T(8,128)}, f32[1024,256]{1,0:T(8,128)})) %all-reduce.17.cloned.1.call-update) | async-done | bytes 2097168 | tf_op jit(solution)/shard_map/psum | solution.py:19
  579.6 33.4 %all-reduce.21.cloned.1.call-done = (f32[1024,256]{1,0:T(8,128)}, f32[1024,256]{1,0:T(8,128)}) async-done(((f32[1024,256]{1,0:T(8,128)}, f32[1024,256]{1,0:T(8,128)}), (f32[1024,256]{1,0:T(8,128)}, f32[1024,256]{1,0:T(8,128)})) %all-reduce.21.cloned.1.call-update) | async-done | bytes 2097168 | tf_op jit(solution)/shard_map/psum | solution.py:19
  616.6 2.3 constant_dynamic-update-slice_fusion
  620.0 99.2 %all-reduce.13.cloned.1.call-done = (f32[1024,256]{1,0:T(8,128)}, f32[1024,256]{1,0:T(8,128)}) async-done(((f32[1024,256]{1,0:T(8,128)}, f32[1024,256]{1,0:T(8,128)}), (f32[1024,256]{1,0:T(8,128)}, f32[1024,256]{1,0:T(8,128)})) %all-reduce.13.cloned.1.call-update) | async-done | bytes 2097168 | tf_op jit(solution)/shard_map/psum | solution.py:89
  719.3 10.9 %fusion.1 = f32[1024,1024]{1,0:T(8,128)} fusion(f32[1024,1024]{1,0:T(8,128)} %constant_dynamic-update-slice_fusion, f32[1024,256]{1,0:T(8,128)} %get-tuple-element.70, f32[1024,256]{1,0:T(8,128)} %get-tuple-element.71, f32[1024,256]{1,0:T(8,128)} %get-tuple-element.62, f32[1024,256]{1,0:T(8,128)} %get-tuple-element.63, s32[1024]{0:T(1024)S(1)} %bitcast.100, ...), kind=kOutput, calls=%fused_computation.9 | convolution fusion | flops 6446645248 | bytes 12591104 | tf_op jit(solution)/shard_map/dot_general | solution.py:28
  730.1 3.3 fusion.17
  733.5 7.6 %reshape.220 = f32[4,1,256,4,1,256]{5,4,3,2,1,0:T(1,128)} reshape(f32[1024,1024]{1,0:T(8,128)} %fusion.17) | data formatting | bytes 8388608 | tf_op jit(solution)/shard_map/reshape | solution.py:105
  (97 shorter events, 41.2 us)
Async XLA Ops:
  6.5 79.8 %all-gather.9.cloned.1.call-start = ((), (), s32[]{:S(2)}) async-start(), calls=%async_computation.1 | async-start | bytes 4456448 | tf_op jit(solution)/shard_map/all_gather | solution.py:13
  24.0 2.0 copy-start
  26.8 118.1 %all-gather.7.cloned.1.call-start = ((), (), s32[]{:S(2)}) async-start(), calls=%async_computation | async-start | bytes 4456448 | tf_op jit(solution)/shard_map/all_gather | solution.py:13
  44.4 1.9 copy-start.2
  47.1 218.4 %all-reduce.19.cloned.1.call-start = ((), (), s32[]{:S(2)}) async-start(), calls=%async_computation.6 | async-start | bytes 4194304 | tf_op jit(solution)/shard_map/psum | solution.py:19
  184.5 114.6 %all-reduce.23.cloned.1.call-start = ((), (), s32[]{:S(2)}) async-start(), calls=%async_computation.8 | async-start | bytes 4194304 | tf_op jit(solution)/shard_map/psum | solution.py:19
  265.5 139.9 %all-reduce.15.cloned.1.call-start = ((), (), s32[]{:S(2)}) async-start(), calls=%async_computation.4 | async-start | bytes 4194304 | tf_op jit(solution)/shard_map/psum | solution.py:89
  301.3 183.5 %all-gather.11.cloned.1.call-start = ((), (), s32[]{:S(2)}) async-start(), calls=%async_computation.2 | async-start | bytes 4456448 | tf_op jit(solution)/shard_map/all_gather | solution.py:13
  416.2 2.0 copy-start.1
  423.1 156.2 %all-reduce.17.cloned.1.call-start = ((), (), s32[]{:S(2)}) async-start(), calls=%async_computation.5 | async-start | bytes 4194304 | tf_op jit(solution)/shard_map/psum | solution.py:19
  450.9 39.2 %copy-start.4 = (f32[128,256]{1,0:T(8,128)}, f32[128,256]{1,0:T(8,128)S(1)}, u32[]{:S(2)}) copy-start(f32[128,256]{1,0:T(8,128)S(1)} %fusion.51) | copy-start | bytes 393220
  490.2 0.7 copy-start.3
  497.1 115.9 %all-reduce.21.cloned.1.call-start = ((), (), s32[]{:S(2)}) async-start(), calls=%async_computation.7 | async-start | bytes 4194304 | tf_op jit(solution)/shard_map/psum | solution.py:19
  579.3 140.0 %all-reduce.13.cloned.1.call-start = ((), (), s32[]{:S(2)}) async-start(), calls=%async_computation.3 | async-start | bytes 4194304 | tf_op jit(solution)/shard_map/psum | solution.py:89
Sparse Core Ops, SparseCore 0:
  26.9 59.3 all-gather.8
  88.7 56.1 all-gather.6
  184.6 80.7 all-reduce.18
  268.0 31.1 all-reduce.22
  302.3 103.0 all-reduce.14
  423.2 61.5 all-gather.10
  497.2 81.9 all-reduce.16
  581.9 31.1 all-reduce.20
  616.4 102.8 all-reduce.12
where the time goes:
time: 749 us; the launch traced here: 748 us
  waiting for transfers between devices  558 us (74%)
  other arithmetic  86.9 us (12%)
  local copies, waits for them, and re-layouts  48.9 us (7%)
  matrix products  38.8 us (5%)
  between operations  13.6 us (2%)
    psum x4, waiting for transfers between devices, from_root(): value = lax.psum(value, axis)  230 us
    psum x2, waiting for transfers between devices, on_device(): lax.psum((jnp.where(keeper, select_columns(got_half), 0.0), jnp.where(kee...  201 us
    all_gather x3, waiting for transfers between devices, picked_2(): lax.all_gather(value, axis)  127 us
    another operation x4, other arithmetic, diagonal_core(): lax.linalg.triangular_solve(diag_factor, identity, left_side=True, lower=...  41.1 us
    dot_general x6, matrix products, product_trans(): lax.dot_general(left, right, (((1,), (1,)), ((), ())), precision=highest,...  28.7 us
    unnamed x4, other arithmetic  28.7 us
  transfers between devices with their start and end apart: 9, of which 9 were waited for; matrix products, arithmetic and copies ran while one was open for 8% of the time, Pallas kernels for 0%

commit v1 on v0

--- a/solution.py
+++ b/solution.py
@@ -16,7 +16,7 @@
 def from_root(value, axes, root):
     value = jnp.where(lax.axis_index(axes) == root, value, jnp.zeros_like(value))
     for axis in axes:
-        value = lax.psum(value, axis)
+        value = jnp.sum(lax.all_gather(value, axis), axis=0)
     return value
 
 

time: 749 us -> 956 us (1.28)
  waiting for transfers between devices: 558 us -> 668 us
  local copies, waits for them, and re-layouts: 48.9 us -> 119 us
  other arithmetic: 86.9 us -> 106 us
    all_gather x0 -> x8, waiting for transfers between devices: none -> 332 us  [from_root(): value = jnp.sum(lax.all_gather(value, axis), axis=0)]
    psum x4 -> x0, waiting for transfers between devices: 230 us -> none  [from_root(): value = lax.psum(value, axis)]
    unnamed x15 -> x30, local copies, waits for them, and re-layouts: 14.5 us -> 57.7 us
    reduce_sum x0 -> x8, other arithmetic: none -> 20.4 us  [from_root(): value = jnp.sum(lax.all_gather(value, axis), axis=0)]
    all_gather x0 -> x4, local copies, waits for them, and re-layouts: none -> 11.6 us  [from_root(): value = jnp.sum(lax.all_gather(value, axis), axis=0)]
  transfers between devices with their start and end apart: 9 -> 13, of which waited for: 9 -> 13; matrix products, arithmetic and copies ran while one was open for 8% -> 18% of each run, Pallas kernels for 0% -> 0%
where the time goes in v1:
time: 956 us; the launch traced here: 948 us
  waiting for transfers between devices  668 us (70%)
  local copies, waits for them, and re-layouts  119 us (12%)
  other arithmetic  106 us (11%)
  matrix products  38 us (4%)
  between operations  14.1 us (1%)
    all_gather x8, waiting for transfers between devices, from_root(): value = jnp.sum(lax.all_gather(value, axis), axis=0)  332 us
    psum x2, waiting for transfers between devices, on_device(): lax.psum((jnp.where(keeper, select_columns(got_half), 0.0), jnp.where(kee...  200 us
    all_gather x3, waiting for transfers between devices, picked_2(): lax.all_gather(value, axis)  135 us
    unnamed x30, local copies, waits for them, and re-layouts  57.7 us
    another operation x4, other arithmetic, diagonal_core(): lax.linalg.triangular_solve(diag_factor, identity, left_side=True, lower=...  41.1 us
    dot_general x6, matrix products, product_trans(): lax.dot_general(left, right, (((1,), (1,)), ((), ())), precision=highest,...  29.2 us
    unnamed x4, other arithmetic  28.6 us
    reduce_sum x8, other arithmetic, from_root(): value = jnp.sum(lax.all_gather(value, axis), axis=0)  20.4 us
  transfers between devices with their start and end apart: 13, of which 13 were waited for; matrix products, arithmetic and copies ran while one was open for 18% of the time, Pallas kernels for 0%

profile of v1, /device:TPU:2, one launch (start us, length us, event | category | flops | bytes accessed | tf_op | source)
XLA Modules:
  0.0 947.6 jit_solution(7994547202168623907)
XLA Ops:
  6.5 14.3 %reduce.10 = f32[4,256,4,256]{3,2,1,0:T(4,128)} reduce(f32[4,1,256,4,1,256]{5,4,3,2,1,0:T(1,128)} %param.8, f32[]{:T(128)} %constant.193), dimensions={1,4}, to_apply=%param.8.reduce_sub_computation | reduce | bytes 8388612 | tf_op args[0]
  20.8 5.1 copy.123
  26.0 5.3 copy.105
  33.0 14.2 %reduce.9 = f32[4,256,4,256]{3,2,1,0:T(4,128)} reduce(f32[4,1,256,4,1,256]{5,4,3,2,1,0:T(1,128)} %param.9, f32[]{:T(128)} %constant.193), dimensions={1,4}, to_apply=%param.9.reduce_sub_computation | reduce | bytes 8388612 | tf_op args[1]
  47.2 3.3 copy.126
  57.8 39.8 %all-gather.25.cloned.1.call-done = f32[4096,256]{0,1:T(8,128)} async-done(((f32[256,256]{0,1:T(8,128)}), f32[4096,256]{0,1:T(8,128)}) %all-gather.25.cloned.1.call-update) | async-done | bytes 4194320 | tf_op jit(solution)/shard_map/all_gather | solution.py:13
  98.7 62.6 %all-gather.23.cloned.1.call-done = f32[4096,256]{0,1:T(8,128)} async-done(((f32[256,256]{0,1:T(8,128)}), f32[4096,256]{0,1:T(8,128)}) %all-gather.23.cloned.1.call-update) | async-done | bytes 4194320 | tf_op jit(solution)/shard_map/all_gather | solution.py:13
  163.2 4.1 while.6
  167.3 19.7 %custom-call.8 = f32[2,128,128]{1,2,0:T(8,128)S(1)} custom-call(f32[2,128,128]{2,1,0:T(8,128)S(1)} %get-tuple-element.44), custom_call_target="InvertDiagBlocksLowerTriangular" | custom-call | tf_op jit(solution)/shard_map/triangular_solve/custom-call.1 | solution.py:35
  193.5 3.7 broadcast_select_fusion.5
  197.4 59.6 %all-gather.31.cloned.1.call-done = f32[8192,256]{0,1:T(8,128)} async-done(((f32[1024,256]{0,1:T(8,128)}), f32[8192,256]{0,1:T(8,128)}) %all-gather.31.cloned.1.call-update) | async-done | bytes 8388624 | tf_op jit(solution)/shard_map/all_gather | solution.py:19
  257.0 10.9 %copy.128 = f32[32,8,8,1024]{3,2,1,0:T(8,128)S(1)} copy(f32[32,8,8,1024]{3,1,2,0:T(8,128)} %bitcast.119) | data formatting | bytes 16777216
  271.3 80.0 %all-gather.27.cloned.1.call-done = f32[8192,256]{0,1:T(8,128)} async-done(((f32[1024,256]{0,1:T(8,128)}), f32[8192,256]{0,1:T(8,128)}) %all-gather.27.cloned.1.call-update) | async-done | bytes 8388624 | tf_op jit(solution)/shard_map/all_gather | solution.py:19
  351.3 10.9 %copy.127 = f32[32,8,8,1024]{3,2,1,0:T(8,128)S(1)} copy(f32[32,8,8,1024]{3,1,2,0:T(8,128)} %bitcast.121) | data formatting | bytes 16777216
  374.7 11.7 %all-gather.29.cloned.1.call-done = f32[2048,256]{0,1:T(8,128)} async-done(((f32[1024,256]{0,1:T(8,128)}), f32[2048,256]{0,1:T(8,128)}) %all-gather.29.cloned.1.call-update) | async-done | bytes 2097168 | tf_op jit(solution)/shard_map/all_gather | solution.py:19
  399.1 99.4 %all-reduce.7.cloned.1.call-done = (f32[1024,256]{0,1:T(8,128)}, f32[1024,256]{0,1:T(8,128)}) async-done(((f32[1024,256]{0,1:T(8,128)}, f32[1024,256]{0,1:T(8,128)}), (f32[1024,256]{0,1:T(8,128)}, f32[1024,256]{0,1:T(8,128)})) %all-reduce.7.cloned.1.call-update) | async-done | bytes 2097168 | tf_op jit(solution)/shard_map/psum | solution.py:89
  498.5 10.8 %fusion = f32[1024,1024]{0,1:T(8,128)} fusion(f32[1024,1024]{0,1:T(8,128)} %copy.105, f32[1024,256]{1,0:T(8,128)S(1)} %reduce_sum.75, f32[1024,256]{1,0:T(8,128)} %reduce_sum.73, f32[1024,256]{0,1:T(8,128)} %get-tuple-element.88, f32[1024,256]{0,1:T(8,128)} %get-tuple-element.89, s32[1024]{0:T(1024)S(1)} %bitcast.133, s32[1024]{0:T(1024)S(1)} %bitcast.135), kind=kOutput, calls=%fused_computation.12 | convolution fusion | flops 6446645248 | bytes 12591104 | tf_op jit(solution)/shard_map/dot_general | solution.py:28
  509.4 3.3 constant_dynamic-update-slice_fusion
  514.7 6.0 while.7
  520.8 19.7 %custom-call.9 = f32[2,128,128]{1,2,0:T(8,128)S(1)} custom-call(f32[2,128,128]{2,1,0:T(8,128)S(1)} %get-tuple-element.45), custom_call_target="InvertDiagBlocksLowerTriangular" | custom-call | tf_op jit(solution)/shard_map/triangular_solve/custom-call.1 | solution.py:35
  542.2 32.9 %all-gather.35.cloned.1.call-done = f32[4096,256]{0,1:T(8,128)} async-done(((f32[256,256]{0,1:T(8,128)}), f32[4096,256]{0,1:T(8,128)}) %all-gather.35.cloned.1.call-update) | async-done | bytes 4194320 | tf_op jit(solution)/shard_map/all_gather | solution.py:13
  583.4 3.4 broadcast_select_fusion.2
  587.1 83.7 %all-gather.41.cloned.1.call-done = f32[8192,256]{0,1:T(8,128)} async-done(((f32[1024,256]{0,1:T(8,128)}), f32[8192,256]{0,1:T(8,128)}) %all-gather.41.cloned.1.call-update) | async-done | bytes 8388624 | tf_op jit(solution)/shard_map/all_gather | solution.py:19
  670.8 10.9 %copy.131 = f32[32,8,8,1024]{3,2,1,0:T(8,128)S(1)} copy(f32[32,8,8,1024]{3,1,2,0:T(8,128)} %bitcast.120) | data formatting | bytes 16777216
  685.1 80.1 %all-gather.37.cloned.1.call-done = f32[8192,256]{0,1:T(8,128)} async-done(((f32[1024,256]{0,1:T(8,128)}), f32[8192,256]{0,1:T(8,128)}) %all-gather.37.cloned.1.call-update) | async-done | bytes 8388624 | tf_op jit(solution)/shard_map/all_gather | solution.py:19
  765.1 10.9 %copy.130 = f32[32,8,8,1024]{3,2,1,0:T(8,128)S(1)} copy(f32[32,8,8,1024]{3,1,2,0:T(8,128)} %bitcast.122) | data formatting | bytes 16777216
  787.6 12.7 %all-gather.39.cloned.1.call-done = f32[2048,256]{0,1:T(8,128)} async-done(((f32[1024,256]{0,1:T(8,128)}), f32[2048,256]{0,1:T(8,128)}) %all-gather.39.cloned.1.call-update) | async-done | bytes 2097168 | tf_op jit(solution)/shard_map/all_gather | solution.py:19
  810.0 100.3 %all-reduce.5.cloned.1.call-done = (f32[1024,256]{0,1:T(8,128)}, f32[1024,256]{0,1:T(8,128)}) async-done(((f32[1024,256]{0,1:T(8,128)}, f32[1024,256]{0,1:T(8,128)}), (f32[1024,256]{0,1:T(8,128)}, f32[1024,256]{0,1:T(8,128)})) %all-reduce.5.cloned.1.call-update) | async-done | bytes 2097168 | tf_op jit(solution)/shard_map/psum | solution.py:89
  910.3 10.5 %fusion.1 = f32[1024,1024]{0,1:T(8,128)} fusion(f32[1024,1024]{0,1:T(8,128)} %get-tuple-element.90, f32[1024,256]{1,0:T(8,128)S(1)} %reduce_sum.79, f32[1024,256]{1,0:T(8,128)S(1)} %reduce_sum.77, f32[1024,256]{0,1:T(8,128)} %get-tuple-element.86, f32[1024,256]{0,1:T(8,128)} %get-tuple-element.87, s32[1024]{0:T(1024)S(1)} %bitcast.134, s32[1024]{0:T(1024)S(1)} %bitcast.136), kind=kOutput, calls=%fused_computation.13 | convolution fusion | flops 6446645248 | bytes 12591104 | tf_op jit(solution)/shard_map/dot_general | solution.py:28
  920.9 3.3 fusion.17
  924.1 5.6 reshape.168
  929.8 10.9 %copy.99 = f32[4,1,256,4,1,256]{5,4,3,2,1,0:T(1,128)} copy(f32[4,1,256,4,1,256]{2,0,5,3,4,1:T(4,128)} %reshape.168) | data formatting | bytes 8388608 | tf_op jit(solution)/shard_map/reshape | solution.py:105
  (146 shorter events, 93.4 us)
Async XLA Ops:
  6.5 91.1 %all-gather.25.cloned.1.call-start = ((), (), s32[]{:S(2)}) async-start(), calls=%async_computation.1 | async-start | bytes 4456448 | tf_op jit(solution)/shard_map/all_gather | solution.py:13
  33.0 128.3 %all-gather.23.cloned.1.call-start = ((), (), s32[]{:S(2)}) async-start(), calls=%async_computation | async-start | bytes 4456448 | tf_op jit(solution)/shard_map/all_gather | solution.py:13
  50.6 1.9 copy-start
  53.4 203.6 %all-gather.31.cloned.1.call-start = ((), (), s32[]{:S(2)}) async-start(), calls=%async_computation.4 | async-start | bytes 9437184 | tf_op jit(solution)/shard_map/all_gather | solution.py:19
  56.9 294.4 %all-gather.27.cloned.1.call-start = ((), (), s32[]{:S(2)}) async-start(), calls=%async_computation.2 | async-start | bytes 9437184 | tf_op jit(solution)/shard_map/all_gather | solution.py:19
  57.7 134.4 %copy-start.6 = (f32[256,256]{1,0:T(8,128)}, f32[256,256]{1,0:T(8,128)S(1)}, u32[]{:S(2)}) copy-start(f32[256,256]{1,0:T(8,128)S(1)} %fusion.39) | copy-start | bytes 786436
  192.3 75.7 %copy-start.5 = (f32[256,256]{0,1:T(8,128)}, f32[256,256]{0,1:T(8,128)S(1)}, u32[]{:S(2)}) copy-start(f32[256,256]{0,1:T(8,128)S(1)} %copy.81) | copy-start | bytes 786436
  197.2 170.4 %all-gather.33.cloned.1.call-start = ((), (), s32[]{:S(2)}) async-start(), calls=%async_computation.5 | async-start | bytes 3145728 | tf_op jit(solution)/shard_map/all_gather | solution.py:19
  271.0 115.4 %all-gather.29.cloned.1.call-start = ((), (), s32[]{:S(2)}) async-start(), calls=%async_computation.3 | async-start | bytes 3145728 | tf_op jit(solution)/shard_map/all_gather | solution.py:19
  365.2 133.3 %all-reduce.7.cloned.1.call-start = ((), (), s32[]{:S(2)}) async-start(), calls=%async_computation.12 | async-start | bytes 4194304 | tf_op jit(solution)/shard_map/psum | solution.py:89
  395.8 179.4 %all-gather.35.cloned.1.call-start = ((), (), s32[]{:S(2)}) async-start(), calls=%async_computation.6 | async-start | bytes 4456448 | tf_op jit(solution)/shard_map/all_gather | solution.py:13
  498.5 10.8 %copy-start.1 = (f32[32,8,4,256]{3,1,2,0:T(8,128)S(1)}, f32[32,8,4,256]{3,1,2,0:T(8,128)}, u32[]{:S(2)}) copy-start(f32[32,8,4,256]{3,1,2,0:T(8,128)} %copy.129) | copy-start | bytes 3145732
  498.5 10.8 %copy-start.2 = (f32[1024,256]{0,1:T(8,128)S(1)}, f32[1024,256]{0,1:T(8,128)}, u32[]{:S(2)}) copy-start(f32[1024,256]{0,1:T(8,128)} %get-tuple-element.101) | copy-start | bytes 3145732
  509.4 31.1 %copy-start.7 = (f32[256,256]{1,0:T(8,128)S(1)}, f32[256,256]{1,0:T(8,128)}, u32[]{:S(2)}) copy-start(f32[256,256]{1,0:T(8,128)} %copy-done.6) | copy-start | bytes 786436
  513.4 157.4 %all-gather.41.cloned.1.call-start = ((), (), s32[]{:S(2)}) async-start(), calls=%async_computation.9 | async-start | bytes 9437184 | tf_op jit(solution)/shard_map/all_gather | solution.py:19
  514.2 251.0 %all-gather.37.cloned.1.call-start = ((), (), s32[]{:S(2)}) async-start(), calls=%async_computation.7 | async-start | bytes 9437184 | tf_op jit(solution)/shard_map/all_gather | solution.py:19
  542.2 38.2 %copy-start.8 = (f32[128,256]{1,0:T(8,128)}, f32[128,256]{1,0:T(8,128)S(1)}, u32[]{:S(2)}) copy-start(f32[128,256]{1,0:T(8,128)S(1)} %fusion.51) | copy-start | bytes 393220
  586.8 194.7 %all-gather.43.cloned.1.call-start = ((), (), s32[]{:S(2)}) async-start(), calls=%async_computation.10 | async-start | bytes 3145728 | tf_op jit(solution)/shard_map/all_gather | solution.py:19
  684.8 115.6 %all-gather.39.cloned.1.call-start = ((), (), s32[]{:S(2)}) async-start(), calls=%async_computation.8 | async-start | bytes 3145728 | tf_op jit(solution)/shard_map/all_gather | solution.py:19
  779.1 131.3 %all-reduce.5.cloned.1.call-start = ((), (), s32[]{:S(2)}) async-start(), calls=%async_computation.11 | async-start | bytes 4194304 | tf_op jit(solution)/shard_map/psum | solution.py:89
  910.3 10.5 %copy-start.3 = (f32[32,8,4,256]{3,1,2,0:T(8,128)S(1)}, f32[32,8,4,256]{3,1,2,0:T(8,128)}, u32[]{:S(2)}) copy-start(f32[32,8,4,256]{3,1,2,0:T(8,128)} %copy.132) | copy-start | bytes 3145732
  910.3 10.5 %copy-start.4 = (f32[1024,256]{0,1:T(8,128)S(1)}, f32[1024,256]{0,1:T(8,128)}, u32[]{:S(2)}) copy-start(f32[1024,256]{0,1:T(8,128)} %get-tuple-element.103) | copy-start | bytes 3145732
Sparse Core Ops, SparseCore 0:
  33.1 64.4 all-gather.24
  100.0 61.2 all-gather.22
  163.1 93.8 all-gather.30
  258.7 92.6 all-gather.26
  353.0 14.4 all-gather.32
  369.2 17.1 all-gather.28
  395.9 102.5 all-reduce.6
  513.6 61.5 all-gather.34
  577.0 93.7 all-gather.40
  672.4 92.6 all-gather.36
  766.9 14.4 all-gather.42
  783.1 17.1 all-gather.38
  807.7 102.6 all-reduce.4
